TPU v7x, 32 devices: a whole 2x2x4 slice. The times are simulated.
32 devices in a mesh: band: 8 (over z, x), slab: 4 (over y, core).
Axes of the slice: x: 2, y: 2, z: 4, core: 2. Of those that a mesh axis runs over, the one named last changes fastest.
Arguments:
- orbitals: float32 [512, 64, 512], P('band', 'slab'), may hold values from -6 to 6
- potential: float32 [64, 512], P('slab'), may hold values from 0 to 1
- projectors: float32 [4, 2048, 128], replicated, may hold values from -0.125 to 0.125
- atom_kind: int32 [32], P('slab'), may hold values from 0 to 3
- atom_plane: int32 [32], P('slab'), may hold values from 0 to 60, as said below
- atom_coef: float32 [32, 128], P('slab'), may hold values from 0.2 to 1
- filter_cut: float32 [1], replicated, may hold values from 0.5 to 2
- filter_top: float32 [1], replicated, may hold values from 9 to 14
Outputs:
- new_orbitals: float32 [512, 32768], P(None, ('slab', 'band'))
Inputs may be any that keep to these rules, and one draw needn't show every extreme that they name: `atom_plane`: block i's 4 planes lie inside the slab of planes (i // 8) * 16 to (i // 8 + 1) * 16 - 1; blocks may share planes.
All inputs are finite; a program needn't handle non-finite values.
Results may differ from a plain program's by a relative error of at most 0.0003.
Values sent between devices are 32-bit elements; how exact they have to be, the bound alone decides.
A program may use at most 128 MiB of HBM per device.

v0:
```python
import jax
import jax.numpy as jnp
from jax import lax
from jax.sharding import PartitionSpec as P

GZ = 32
ORDER = 6
low_edge = -1.0
near_coef = 4.0 / 3.0
far_coef = -1.0 / 12.0
self_coef = -2.5
highest = lax.Precision.HIGHEST


def padded_2(value, sides, width):
    for axis, dim in sides:
        size, length = (lax.axis_size(axis), value.shape[dim])
        up = [(i, (i + 1) % size) for i in range(size)]
        down = [(j, i) for i, j in up]
        last = lax.slice_in_dim(value, length - width, length, axis=dim)
        first = lax.slice_in_dim(value, 0, width, axis=dim)
        before = lax.ppermute(last, axis, up)
        after = lax.ppermute(first, axis, down)
        value = jnp.concatenate([before, value, after], axis=dim)
    return value


def shifted(source, offset):
    if offset > 0:
        zeros_part = jnp.zeros(source.shape[:-1] + (offset,), source.dtype)
        return jnp.concatenate([zeros_part, source[..., :-offset]], axis=-1)
    zeros_part = jnp.zeros(source.shape[:-1] + (-offset,), source.dtype)
    return jnp.concatenate([source[..., -offset:], zeros_part], axis=-1)


def transverse(source, width_z):
    length_last = source.shape[-1]
    z_position = jnp.arange(length_last) % width_z
    result_sum = 2.0 * self_coef * source
    for offset, weight_coef in ((1, near_coef), (-1, near_coef), (2, far_coef), (-2, far_coef)):
        result_sum = result_sum + weight_coef * shifted(source, offset * width_z)
        inside = (z_position - offset >= 0) & (z_position - offset < width_z)
        result_sum = result_sum + weight_coef * jnp.where(inside, shifted(source, offset), 0.0)
    return result_sum


def local(
    orbitals, potential, projectors, atom_kind, atom_plane, atom_coef, filter_cut, filter_top
):
    band_count, planes, points = orbitals.shape
    kind_count, block_pts, func_count = projectors.shape
    atom_count = atom_kind.shape[0]
    block_depth = block_pts // points
    local_plane = atom_plane - lax.axis_index("slab") * planes
    plane_ids = jnp.arange(planes)
    depth_ids = jnp.arange(block_depth)
    selector = (
        plane_ids[None, None, :] == local_plane[:, None, None] + depth_ids[None, :, None]
    ).astype(jnp.float32)
    atom_tables = jnp.take(projectors, atom_kind, axis=0)
    coef_rows = atom_coef[:, None, :]

    def hamiltonian_fn(source):
        padded = padded_2(source, (("slab", 1),), 2)
        along_x = self_coef * source
        along_x = along_x + near_coef * (padded[:, 1 : planes + 1] + padded[:, 3 : planes + 3])
        along_x = along_x + far_coef * (padded[:, 0:planes] + padded[:, 4 : planes + 4])
        laplace = along_x + transverse(source, GZ)
        blocks = jnp.einsum("ajx,nxp->anjp", selector, source, precision=highest)
        blocks = blocks.reshape(atom_count, band_count, block_pts)
        coupled = jnp.einsum("anq,aqf->anf", blocks, atom_tables, precision=highest) * coef_rows
        spread_back = jnp.einsum("anf,aqf->anq", coupled, atom_tables, precision=highest)
        spread_back = spread_back.reshape(atom_count, band_count, block_depth, points)
        nonlocal_part = jnp.einsum("ajx,anjp->nxp", selector, spread_back, precision=highest)
        return -0.5 * laplace + potential[None] * source + nonlocal_part

    cut_value = filter_cut[0]
    top_value = filter_top[0]
    half_width = (top_value - cut_value) / 2.0
    centre = (top_value + cut_value) / 2.0
    sigma_now = half_width / (low_edge - centre)
    tau_value = 2.0 / sigma_now
    previous = orbitals
    current = (hamiltonian_fn(previous) - centre * previous) * (sigma_now / half_width)
    for step_index in range(ORDER - 1):
        sigma_next = 1.0 / (tau_value - sigma_now)
        upcoming = (hamiltonian_fn(current) - centre * current) * (
            2.0 * sigma_next / half_width
        ) - sigma_now * sigma_next * previous
        previous = current
        current = upcoming
        sigma_now = sigma_next
    flat_orbitals = current.reshape(band_count, planes * points)
    grid_layout = lax.all_to_all(flat_orbitals, "band", split_axis=1, concat_axis=0, tiled=True)
    point_total = grid_layout.shape[1] * lax.axis_size(("band", "slab"))
    partial_gram = jnp.dot(grid_layout, grid_layout.T, precision=highest) / point_total
    gram_matrix = lax.psum(partial_gram, ("band", "slab"))
    factor = jnp.linalg.cholesky(gram_matrix)
    return jax.scipy.linalg.solve_triangular(factor, grid_layout, lower=True)


def solution(mesh):
    in_specs = (
        P("band", "slab", None),
        P("slab", None),
        P(),
        P("slab"),
        P("slab"),
        P("slab", None),
        P(),
        P(),
    )
    out_specs = P(None, ("slab", "band"))
    return jax.shard_map(local, mesh=mesh, in_specs=in_specs, out_specs=out_specs, check_vma=False)
```

profile of v0, /device:TPU:0, one launch (start us, length us, event | category | flops | bytes accessed | tf_op | source)
XLA Modules:
  0.0 782.5 jit_solution(11253992471097181108)
XLA Ops:
  31.2 6.9 copy.17
  38.1 6.3 reshape.122
  44.4 6.6 gather_fusion
  51.0 10.4 %convolution_multiply_fusion.6 = f32[8,64,128]{2,1,0:T(8,128)S(1)} fusion(f32[8,64,2048]{2,1,0:T(8,128)} %reshape.122, f32[8,128]{1,0:T(8,128)S(1)} %copy-done.24, f32[8,2048,128]{2,1,0:T(8,128)} %gather_fusion, pred[8]{0:T(512)(128)(4,1)S(1)} %compare_and_fusion), kind=kOutput, calls=%fused_computation.154 | convolution fusion | flops 1612775424 | bytes 12849160 | tf_op jit(solution)/shard_map/anq,aqf->anf/dot_general | solution.py:71
  61.5 10.5 %fusion.153 = f32[8,64,2048]{2,1,0:T(8,128)} fusion(f32[8,64,128]{2,1,0:T(8,128)S(1)} %convolution_multiply_fusion.6, f32[8,2048,128]{2,1,0:T(8,128)S(1)} %copy-done, pred[8]{0:T(512)(128)(4,1)S(1)} %compare_and_fusion), kind=kOutput, calls=%fused_computation.243 | convolution fusion | flops 1612709888 | bytes 12845064 | tf_op jit(solution)/shard_map/anf,aqf->anq/dot_general | solution.py:72
  81.7 12.0 %fusion.75 = f32[64,16,512]{2,1,0:T(8,128)S(1)} fusion(f32[64,2,512]{2,1,0:T(2,128)S(1)} %collective-permute-done, f32[64,16,512]{2,1,0:T(8,128)S(1)} %copy-done.1, f32[64,18,512]{2,1,0:T(8,128)} %copy-done.23, f32[64,16,510]{2,1,0:T(8,128)} %get-tuple-element.84, f32[64,16,448]{2,1,0:T(8,128)} %get-tuple-element.82, ...), kind=kOutput, calls=%fused_computation.107 | convolution fusion | flops 221249536 | bytes 28846600 | tf_op jit(solution)/shard_map/ajx,anjp->nxp/dot_general | solution.py:74
  115.4 9.3 %convolution_multiply_fusion.5 = f32[8,64,128]{2,1,0:T(8,128)S(1)} fusion(f32[8,64,2048]{2,1,0:T(8,128)} %reshape.124, f32[8,128]{1,0:T(8,128)S(1)} %copy-done.24, f32[8,2048,128]{2,1,0:T(8,128)} %gather_fusion, pred[8]{0:T(512)(128)(4,1)S(1)} %compare_and_fusion), kind=kOutput, calls=%fused_computation.153 | convolution fusion | flops 1612775424 | bytes 12849160 | tf_op jit(solution)/shard_map/anq,aqf->anf/dot_general | solution.py:71
  124.7 12.7 %fusion.152 = f32[8,64,2048]{2,1,0:T(8,128)} fusion(f32[8,64,128]{2,1,0:T(8,128)S(1)} %convolution_multiply_fusion.5, f32[8,2048,128]{2,1,0:T(8,128)} %gather_fusion, pred[8]{0:T(512)(128)(4,1)S(1)} %compare_and_fusion), kind=kOutput, calls=%fused_computation.242 | convolution fusion | flops 1612709888 | bytes 12845064 | tf_op jit(solution)/shard_map/anf,aqf->anq/dot_general | solution.py:72
  150.8 12.0 %fusion.63 = f32[64,16,512]{2,1,0:T(8,128)S(1)} fusion(f32[64,16,512]{2,1,0:T(8,128)S(1)} %copy-done.9, f32[64,2,512]{2,1,0:T(2,128)S(1)} %collective-permute-done.3, f32[64,2,512]{2,1,0:T(2,128)S(1)} %collective-permute-done.2, f32[64,16,512]{2,1,0:T(8,128)S(1)} %copy-done.1, f32[64,16,510]{2,1,0:T(8,128)} %get-tuple-element.74, ...), kind=kOutput, calls=%fused_computation.95 | convolution fusion | flops 223346688 | bytes 27011596 | tf_op jit(solution)/shard_map/ajx,anjp->nxp/dot_general | solution.py:74
  184.6 9.1 %convolution_multiply_fusion.4 = f32[8,64,128]{2,1,0:T(8,128)S(1)} fusion(f32[8,64,2048]{2,1,0:T(8,128)} %reshape.126, f32[8,128]{1,0:T(8,128)S(1)} %copy-done.24, f32[8,2048,128]{2,1,0:T(8,128)} %gather_fusion, pred[8]{0:T(512)(128)(4,1)S(1)} %compare_and_fusion), kind=kOutput, calls=%fused_computation.152 | convolution fusion | flops 1612775424 | bytes 12849160 | tf_op jit(solution)/shard_map/anq,aqf->anf/dot_general | solution.py:71
  193.7 12.7 %fusion.151 = f32[8,64,2048]{2,1,0:T(8,128)} fusion(f32[8,64,128]{2,1,0:T(8,128)S(1)} %convolution_multiply_fusion.4, f32[8,2048,128]{2,1,0:T(8,128)} %gather_fusion, pred[8]{0:T(512)(128)(4,1)S(1)} %compare_and_fusion), kind=kOutput, calls=%fused_computation.241 | convolution fusion | flops 1612709888 | bytes 12845064 | tf_op jit(solution)/shard_map/anf,aqf->anq/dot_general | solution.py:72
  220.0 12.3 %fusion.50 = f32[64,16,512]{2,1,0:T(8,128)S(1)} fusion(f32[64,16,512]{2,1,0:T(8,128)S(1)} %copy-done.6, f32[64,2,512]{2,1,0:T(2,128)S(1)} %collective-permute-done.5, f32[64,2,512]{2,1,0:T(2,128)S(1)} %collective-permute-done.4, f32[64,16,512]{2,1,0:T(8,128)S(1)} %copy-done.10, f32[64,16,510]{2,1,0:T(8,128)} %get-tuple-element.64, ...), kind=kOutput, calls=%fused_computation.82 | convolution fusion | flops 223346688 | bytes 27011596 | tf_op jit(solution)/shard_map/ajx,anjp->nxp/dot_general | solution.py:74
  254.0 9.0 %convolution_multiply_fusion.3 = f32[8,64,128]{2,1,0:T(8,128)S(1)} fusion(f32[8,64,2048]{2,1,0:T(8,128)} %reshape.128, f32[8,128]{1,0:T(8,128)S(1)} %copy-done.24, f32[8,2048,128]{2,1,0:T(8,128)} %gather_fusion, pred[8]{0:T(512)(128)(4,1)S(1)} %compare_and_fusion), kind=kOutput, calls=%fused_computation.151 | convolution fusion | flops 1612775424 | bytes 12849160 | tf_op jit(solution)/shard_map/anq,aqf->anf/dot_general | solution.py:71
  263.0 12.7 %fusion.150 = f32[8,64,2048]{2,1,0:T(8,128)} fusion(f32[8,64,128]{2,1,0:T(8,128)S(1)} %convolution_multiply_fusion.3, f32[8,2048,128]{2,1,0:T(8,128)} %gather_fusion, pred[8]{0:T(512)(128)(4,1)S(1)} %compare_and_fusion), kind=kOutput, calls=%fused_computation.240 | convolution fusion | flops 1612709888 | bytes 12845064 | tf_op jit(solution)/shard_map/anf,aqf->anq/dot_general | solution.py:72
  289.2 13.8 %fusion.37 = f32[64,16,512]{2,1,0:T(8,128)S(1)} fusion(f32[64,16,512]{2,1,0:T(8,128)} %copy-done.2, f32[64,2,512]{2,1,0:T(2,128)S(1)} %collective-permute-done.7, f32[64,2,512]{2,1,0:T(2,128)S(1)} %collective-permute-done.6, f32[64,16,512]{2,1,0:T(8,128)S(1)} %copy-done.7, f32[64,16,510]{2,1,0:T(8,128)} %get-tuple-element.54, ...), kind=kOutput, calls=%fused_computation.69 | convolution fusion | flops 223346688 | bytes 27011596 | tf_op jit(solution)/shard_map/ajx,anjp->nxp/dot_general | solution.py:74
  324.6 9.3 %convolution_multiply_fusion.2 = f32[8,64,128]{2,1,0:T(8,128)S(1)} fusion(f32[8,64,2048]{2,1,0:T(8,128)} %reshape.130, f32[8,128]{1,0:T(8,128)S(1)} %copy-done.24, f32[8,2048,128]{2,1,0:T(8,128)} %gather_fusion, pred[8]{0:T(512)(128)(4,1)S(1)} %compare_and_fusion), kind=kOutput, calls=%fused_computation.150 | convolution fusion | flops 1612775424 | bytes 12849160 | tf_op jit(solution)/shard_map/anq,aqf->anf/dot_general | solution.py:71
  333.8 12.7 %fusion.149 = f32[8,64,2048]{2,1,0:T(8,128)} fusion(f32[8,64,128]{2,1,0:T(8,128)S(1)} %convolution_multiply_fusion.2, f32[8,2048,128]{2,1,0:T(8,128)} %gather_fusion, pred[8]{0:T(512)(128)(4,1)S(1)} %compare_and_fusion), kind=kOutput, calls=%fused_computation.239 | convolution fusion | flops 1612709888 | bytes 12845064 | tf_op jit(solution)/shard_map/anf,aqf->anq/dot_general | solution.py:72
  359.9 12.0 %fusion.24 = f32[64,16,512]{2,1,0:T(8,128)S(1)} fusion(f32[64,16,512]{2,1,0:T(8,128)S(1)} %fusion.37, f32[64,2,512]{2,1,0:T(2,128)S(1)} %collective-permute-done.9, f32[64,2,512]{2,1,0:T(2,128)S(1)} %collective-permute-done.8, f32[64,16,512]{2,1,0:T(8,128)S(1)} %copy-done.3, f32[64,16,510]{2,1,0:T(8,128)} %get-tuple-element.44, ...), kind=kOutput, calls=%fused_computation.56 | convolution fusion | flops 223346688 | bytes 27011596 | tf_op jit(solution)/shard_map/ajx,anjp->nxp/dot_general | solution.py:74
  393.5 9.3 %convolution_multiply_fusion.1 = f32[8,64,128]{2,1,0:T(8,128)S(1)} fusion(f32[8,64,2048]{2,1,0:T(8,128)} %reshape.132, f32[8,128]{1,0:T(8,128)S(1)} %copy-done.24, f32[8,2048,128]{2,1,0:T(8,128)} %gather_fusion, pred[8]{0:T(512)(128)(4,1)S(1)} %compare_and_fusion), kind=kOutput, calls=%fused_computation.149 | convolution fusion | flops 1612775424 | bytes 12849160 | tf_op jit(solution)/shard_map/anq,aqf->anf/dot_general | solution.py:71
  402.8 12.8 %fusion.148 = f32[8,64,2048]{2,1,0:T(8,128)} fusion(f32[8,64,128]{2,1,0:T(8,128)S(1)} %convolution_multiply_fusion.1, f32[8,2048,128]{2,1,0:T(8,128)} %gather_fusion, pred[8]{0:T(512)(128)(4,1)S(1)} %compare_and_fusion), kind=kOutput, calls=%fused_computation.238 | convolution fusion | flops 1612709888 | bytes 12845064 | tf_op jit(solution)/shard_map/anf,aqf->anq/dot_general | solution.py:72
  428.9 12.5 %fusion.11 = f32[64,16,512]{2,1,0:T(8,128)} fusion(f32[64,16,512]{2,1,0:T(8,128)S(1)} %copy-done.12, f32[64,2,512]{2,1,0:T(2,128)S(1)} %collective-permute-done.11, f32[64,2,512]{2,1,0:T(2,128)S(1)} %collective-permute-done.10, f32[64,16,512]{2,1,0:T(8,128)S(1)} %fusion.37, f32[64,16,510]{2,1,0:T(8,128)} %get-tuple-element.34, ...), kind=kOutput, calls=%fused_computation.43 | convolution fusion | flops 223346688 | bytes 27011596 | tf_op jit(solution)/shard_map/ajx,anjp->nxp/dot_general | solution.py:74
  444.5 55.2 %all_to_all.19 = f32[64,8,1024]{2,0,1:T(8,128)S(1)} all-to-all(f32[64,8,1024]{2,0,1:T(8,128)S(1)} %copy.29), channel_id=1, replica_groups=mesh['band'=8,'slab'=4] {'band'}, dimensions={1} | all-to-all | bytes 4194304 | tf_op jit(solution)/shard_map/all_to_all | solution.py:94
  505.5 128.1 %all-reduce.51.cloned.1.call-done = f32[512,512]{0,1:T(8,128)} async-done(((f32[512,512]{0,1:T(8,128)}), f32[512,512]{0,1:T(8,128)}) %all-reduce.51.cloned.1.call-update) | async-done | bytes 1048592 | tf_op jit(solution)/shard_map/psum | solution.py:97
  635.5 11.7 %cholesky.104 = f32[128,128]{1,0:T(8,128)S(1)} custom-call(f32[128,128]{1,0:T(8,128)S(1)} %cholesky.266), custom_call_target="Cholesky" | custom-call | tf_op jit(solution)/shard_map/jit(cholesky)/cholesky | solution.py:98
  647.4 9.8 %custom-call.31 = f32[1,128,128]{1,2,0:T(8,128)S(1)} custom-call(f32[1,128,128]{2,1,0:T(8,128)S(1)} %get-tuple-element.96), custom_call_target="InvertDiagBlocksLowerTriangular" | custom-call | tf_op jit(solution)/shard_map/jit(cholesky)/cholesky | solution.py:98
  657.9 11.9 %cholesky.217 = f32[128,128]{1,0:T(8,128)S(1)} custom-call(f32[128,128]{1,0:T(8,128)S(1)} %cholesky.270), custom_call_target="Cholesky" | custom-call | tf_op jit(solution)/shard_map/jit(cholesky)/cholesky | solution.py:98
  671.2 9.8 %custom-call.32 = f32[1,128,128]{1,2,0:T(8,128)S(1)} custom-call(f32[1,128,128]{2,1,0:T(8,128)S(1)} %get-tuple-element.93), custom_call_target="InvertDiagBlocksLowerTriangular" | custom-call | tf_op jit(solution)/shard_map/jit(cholesky)/cholesky | solution.py:98
  681.7 11.7 %cholesky.238 = f32[128,128]{1,0:T(8,128)S(1)} custom-call(f32[128,128]{1,0:T(8,128)S(1)} %cholesky.275), custom_call_target="Cholesky" | custom-call | tf_op jit(solution)/shard_map/jit(cholesky)/cholesky | solution.py:98
  694.1 9.8 %custom-call.33 = f32[1,128,128]{1,2,0:T(8,128)S(1)} custom-call(f32[1,128,128]{2,1,0:T(8,128)S(1)} %get-tuple-element.90), custom_call_target="InvertDiagBlocksLowerTriangular" | custom-call | tf_op jit(solution)/shard_map/jit(cholesky)/cholesky | solution.py:98
  704.5 11.9 %cholesky.255 = f32[128,128]{1,0:T(8,128)S(1)} custom-call(f32[128,128]{1,0:T(8,128)S(1)} %convolution_subtract_fusion.4), custom_call_target="Cholesky" | custom-call | tf_op jit(solution)/shard_map/jit(cholesky)/cholesky | solution.py:98
  719.9 8.4 %while.1 = (s32[]{:T(128)}, f32[512,512]{1,0:T(8,128)S(1)}, s32[4,2]{0,1:T(2,128)S(1)}, f32[4,128,128]{2,1,0:T(8,128)S(1)}, s32[]{:T(128)}) while((s32[]{:T(128)}, f32[512,512]{1,0:T(8,128)S(1)}, s32[4,2]{0,1:T(2,128)S(1)}, f32[4,128,128]{2,1,0:T(8,128)S(1)}, s32[]{:T(128)}) %tuple.61), condition=%wide.while_cond, body=%wide.while_body.sunk | while | flops 2 | bytes 131181 | solution.py:99
  728.3 39.3 %custom-call.34 = f32[4,128,128]{1,2,0:T(8,128)S(1)} custom-call(f32[4,128,128]{2,1,0:T(8,128)S(1)} %get-tuple-element.12), custom_call_target="InvertDiagBlocksLowerTriangular" | custom-call | tf_op jit(solution)/shard_map/jit(_solve_triangular)/triangular_solve | solution.py:99
  (188 shorter events, 239.3 us)
Async XLA Ops:
  6.5 627.1 %all-reduce.51.cloned.1.call-start = ((), (), s32[]{:S(2)}) async-start(), calls=%async_computation.1 | async-start | bytes 2097152 | tf_op jit(solution)/shard_map/psum | solution.py:97
  8.3 70.2 %collective-permute-start.1 = (f32[64,2,512]{2,1,0:T(2,128)S(1)}, f32[64,2,512]{2,1,0:T(2,128)S(1)}, u32[]{:S(2)}, u32[]{:S(2)}) collective-permute-start(f32[64,2,512]{2,1,0:T(2,128)S(1)} %get-tuple-element.85), channel_id=1, source_target_pairs={{1,0},{2,1},{3,2},{0,3},{5,4},{6,5},{7,6},{4,7},{9,8},{10,9},{11,1... | collective-permute-start | bytes 786440 | tf_op jit(solution)/shard_map/ppermute | solution.py:23
  10.8 67.9 %collective-permute-start = (f32[64,2,512]{2,1,0:T(2,128)S(1)}, f32[64,2,512]{2,1,0:T(2,128)S(1)}, u32[]{:S(2)}, u32[]{:S(2)}) collective-permute-start(f32[64,2,512]{2,1,0:T(2,128)S(1)} %get-tuple-element.86), channel_id=1, source_target_pairs={{0,1},{1,2},{2,3},{3,0},{4,5},{5,6},{6,7},{7,4},{8,9},{9,10},{10,1... | collective-permute-start | bytes 786440 | tf_op jit(solution)/shard_map/ppermute | solution.py:22
  44.4 6.6 copy-start.24
  51.0 10.4 %copy-start = (f32[8,2048,128]{2,1,0:T(8,128)S(1)}, f32[8,2048,128]{2,1,0:T(8,128)}, u32[]{:S(2)}) copy-start(f32[8,2048,128]{2,1,0:T(8,128)} %gather_fusion) | copy-start | bytes 25165828
  93.7 10.6 %copy-start.8 = (f32[64,16,512]{2,1,0:T(8,128)}, f32[64,16,512]{2,1,0:T(8,128)S(1)}, u32[]{:S(2)}) copy-start(f32[64,16,512]{2,1,0:T(8,128)S(1)} %fusion.75) | copy-start | bytes 6291460
  143.5 7.2 collective-permute-start.2
  144.2 6.5 copy-start.9
  144.2 6.5 copy-start.19
  144.3 6.5 collective-permute-start.3
  162.8 10.7 %copy-start.4 = (f32[64,16,512]{2,1,0:T(8,128)}, f32[64,16,512]{2,1,0:T(8,128)S(1)}, u32[]{:S(2)}) copy-start(f32[64,16,512]{2,1,0:T(8,128)S(1)} %fusion.63) | copy-start | bytes 6291460
  206.4 8.2 %copy-start.5 = (f32[64,16,512]{2,1,0:T(8,128)S(1)}, f32[64,16,512]{2,1,0:T(8,128)}, u32[]{:S(2)}) copy-start(f32[64,16,512]{2,1,0:T(8,128)} %copy-done.4) | copy-start | bytes 6291460
  212.6 7.4 collective-permute-start.4
  213.8 6.2 copy-start.6
  213.8 6.2 copy-start.10
  213.8 6.2 copy-start.17
  213.8 6.2 collective-permute-start.5
  232.3 51.4 %copy-start.2 = (f32[64,16,512]{2,1,0:T(8,128)}, f32[64,16,512]{2,1,0:T(8,128)S(1)}, u32[]{:S(2)}) copy-start(f32[64,16,512]{2,1,0:T(8,128)S(1)} %fusion.50) | copy-start | bytes 6291460
  281.8 7.4 collective-permute-start.6
  283.0 6.2 copy-start.7
  283.0 6.2 copy-start.16
  283.0 6.2 collective-permute-start.7
  352.6 7.3 collective-permute-start.8
  353.7 6.2 copy-start.3
  353.7 6.2 copy-start.18
  353.7 6.1 collective-permute-start.9
  371.9 10.6 %copy-start.11 = (f32[64,16,512]{2,1,0:T(8,128)}, f32[64,16,512]{2,1,0:T(8,128)S(1)}, u32[]{:S(2)}) copy-start(f32[64,16,512]{2,1,0:T(8,128)S(1)} %fusion.24) | copy-start | bytes 6291460
  421.6 7.2 collective-permute-start.10
  422.8 6.1 copy-start.15
  422.8 6.1 collective-permute-start.11
  716.4 52.9 %copy-start.21 = (f32[2,64,1024]{2,1,0:T(8,128)S(1)}, f32[2,64,1024]{2,1,0:T(8,128)}, u32[]{:S(2)}) copy-start(f32[2,64,1024]{2,1,0:T(8,128)} %get-tuple-element.25) | copy-start | bytes 1572868
  728.3 42.3 %copy-start.20 = (f32[2,64,1024]{2,1,0:T(8,128)S(1)}, f32[2,64,1024]{2,1,0:T(8,128)}, u32[]{:S(2)}) copy-start(f32[2,64,1024]{2,1,0:T(8,128)} %get-tuple-element.24) | copy-start | bytes 1572868
  (7 other events, 23.7 us)
Sparse Core Ops, SparseCore 0:
  504.3 129.2 all-reduce.50
where the time goes:
time: 790 us; the launch traced here: 783 us
  matrix products  234 us (30%)
  local copies, waits for them, and re-layouts  203 us (26%)
  waiting for transfers between devices  137 us (17%)
  other arithmetic  123 us (16%)
  blocking collectives  55.2 us (7%)
  between operations  18.9 us (2%)
  starting transfers between devices  11.8 us (1%)
    psum x1, waiting for transfers between devices, local(): gram_matrix = lax.psum(partial_gram, ('band', 'slab'))  128 us
    another operation x15, other arithmetic, local(): factor = jnp.linalg.cholesky(gram_matrix)  79.5 us
    dot_general x6, matrix products, hamiltonian_fn(): jnp.einsum('ajx,anjp->nxp', selector, spread_back, precision=highest)  74.6 us
    dot_general x6, matrix products, hamiltonian_fn(): jnp.einsum('anf,aqf->anq', coupled, atom_tables, precision=highest)  74.1 us
    slice x24, local copies, waits for them, and re-layouts, shifted(): return jnp.concatenate([zeros_part, source[..., :-offset]], axis=-1)  71.5 us
    dot_general x6, matrix products, hamiltonian_fn(): jnp.einsum('anq,aqf->anf', blocks, atom_tables, precision=highest)  56.4 us
    all_to_all x1, blocking collectives, local(): lax.all_to_all(flat_orbitals, 'band', split_axis=1, concat_axis=0, tiled=...  55.2 us
    another operation x4, other arithmetic, local(): return jax.scipy.linalg.solve_triangular(factor, grid_layout, lower=True)  41 us
  transfers between devices with their start and end apart: 13, of which 6 were waited for; matrix products, arithmetic and copies ran while one was open for 11% of the time, Pallas kernels for 0%

commit v1 on v0

--- a/solution.py
+++ b/solution.py
@@ -94,7 +94,7 @@
     grid_layout = lax.all_to_all(flat_orbitals, "band", split_axis=1, concat_axis=0, tiled=True)
     point_total = grid_layout.shape[1] * lax.axis_size(("band", "slab"))
     partial_gram = jnp.dot(grid_layout, grid_layout.T, precision=highest) / point_total
-    gram_matrix = lax.psum(partial_gram, ("band", "slab"))
+    gram_matrix = lax.psum(lax.psum(partial_gram, "slab"), "band")
     factor = jnp.linalg.cholesky(gram_matrix)
     return jax.scipy.linalg.solve_triangular(factor, grid_layout, lower=True)
 

time: 790 us -> 778 us (0.985)
  waiting for transfers between devices: 137 us -> 124 us
    psum x1 -> x2, waiting for transfers between devices: 128 us -> 116 us  [local(): gram_matrix = lax.psum(lax.psum(partial_gram, 'slab'), 'band')]
  transfers between devices with their start and end apart: 13 -> 14, of which waited for: 6 -> 7; matrix products, arithmetic and copies ran while one was open for 11% -> 11% of each run, Pallas kernels for 0% -> 0%
where the time goes in v1:
time: 778 us; the launch traced here: 770 us
  matrix products  234 us (30%)
  local copies, waits for them, and re-layouts  203 us (26%)
  waiting for transfers between devices  124 us (16%)
  other arithmetic  123 us (16%)
  blocking collectives  55.2 us (7%)
  between operations  18.9 us (2%)
  starting transfers between devices  12 us (2%)
    psum x2, waiting for transfers between devices, local(): gram_matrix = lax.psum(lax.psum(partial_gram, 'slab'), 'band')  116 us
    another operation x15, other arithmetic, local(): factor = jnp.linalg.cholesky(gram_matrix)  79.6 us
    dot_general x6, matrix products, hamiltonian_fn(): jnp.einsum('ajx,anjp->nxp', selector, spread_back, precision=highest)  75 us
    dot_general x6, matrix products, hamiltonian_fn(): jnp.einsum('anf,aqf->anq', coupled, atom_tables, precision=highest)  74.1 us
    slice x24, local copies, waits for them, and re-layouts, shifted(): return jnp.concatenate([zeros_part, source[..., :-offset]], axis=-1)  71.5 us
    dot_general x6, matrix products, hamiltonian_fn(): jnp.einsum('anq,aqf->anf', blocks, atom_tables, precision=highest)  56.2 us
    all_to_all x1, blocking collectives, local(): lax.all_to_all(flat_orbitals, 'band', split_axis=1, concat_axis=0, tiled=...  55.2 us
    another operation x4, other arithmetic, local(): return jax.scipy.linalg.solve_triangular(factor, grid_layout, lower=True)  41 us
  transfers between devices with their start and end apart: 14, of which 7 were waited for; matrix products, arithmetic and copies ran while one was open for 11% of the time, Pallas kernels for 0%

profile of v1, /device:TPU:0, one launch (start us, length us, event | category | flops | bytes accessed | tf_op | source)
XLA Modules:
  0.0 770.5 jit_solution(2498419455078202497)
XLA Ops:
  31.2 6.9 copy.17
  44.4 6.6 gather_fusion
  51.0 10.4 %convolution_multiply_fusion.6 = f32[8,64,128]{2,1,0:T(8,128)S(1)} fusion(f32[8,64,2048]{2,1,0:T(8,128)} %reshape.122, f32[8,128]{1,0:T(8,128)S(1)} %copy-done.24, f32[8,2048,128]{2,1,0:T(8,128)} %gather_fusion, pred[8]{0:T(512)(128)(4,1)S(1)} %compare_and_fusion), kind=kOutput, calls=%fused_computation.154 | convolution fusion | flops 1612775424 | bytes 12849160 | tf_op jit(solution)/shard_map/anq,aqf->anf/dot_general | solution.py:71
  61.5 10.5 %fusion.153 = f32[8,64,2048]{2,1,0:T(8,128)} fusion(f32[8,64,128]{2,1,0:T(8,128)S(1)} %convolution_multiply_fusion.6, f32[8,2048,128]{2,1,0:T(8,128)S(1)} %copy-done, pred[8]{0:T(512)(128)(4,1)S(1)} %compare_and_fusion), kind=kOutput, calls=%fused_computation.243 | convolution fusion | flops 1612709888 | bytes 12845064 | tf_op jit(solution)/shard_map/anf,aqf->anq/dot_general | solution.py:72
  81.7 12.0 %fusion.75 = f32[64,16,512]{2,1,0:T(8,128)S(1)} fusion(f32[64,2,512]{2,1,0:T(2,128)S(1)} %collective-permute-done, f32[64,16,512]{2,1,0:T(8,128)S(1)} %copy-done.1, f32[64,18,512]{2,1,0:T(8,128)} %copy-done.23, f32[64,16,510]{2,1,0:T(8,128)} %get-tuple-element.84, f32[64,16,448]{2,1,0:T(8,128)} %get-tuple-element.82, ...), kind=kOutput, calls=%fused_computation.107 | convolution fusion | flops 221249536 | bytes 28846600 | tf_op jit(solution)/shard_map/ajx,anjp->nxp/dot_general | solution.py:74
  115.4 9.3 %convolution_multiply_fusion.5 = f32[8,64,128]{2,1,0:T(8,128)S(1)} fusion(f32[8,64,2048]{2,1,0:T(8,128)} %reshape.124, f32[8,128]{1,0:T(8,128)S(1)} %copy-done.24, f32[8,2048,128]{2,1,0:T(8,128)} %gather_fusion, pred[8]{0:T(512)(128)(4,1)S(1)} %compare_and_fusion), kind=kOutput, calls=%fused_computation.153 | convolution fusion | flops 1612775424 | bytes 12849160 | tf_op jit(solution)/shard_map/anq,aqf->anf/dot_general | solution.py:71
  124.7 12.7 %fusion.152 = f32[8,64,2048]{2,1,0:T(8,128)} fusion(f32[8,64,128]{2,1,0:T(8,128)S(1)} %convolution_multiply_fusion.5, f32[8,2048,128]{2,1,0:T(8,128)} %gather_fusion, pred[8]{0:T(512)(128)(4,1)S(1)} %compare_and_fusion), kind=kOutput, calls=%fused_computation.242 | convolution fusion | flops 1612709888 | bytes 12845064 | tf_op jit(solution)/shard_map/anf,aqf->anq/dot_general | solution.py:72
  150.8 12.0 %fusion.63 = f32[64,16,512]{2,1,0:T(8,128)S(1)} fusion(f32[64,16,512]{2,1,0:T(8,128)S(1)} %copy-done.9, f32[64,2,512]{2,1,0:T(2,128)S(1)} %collective-permute-done.3, f32[64,2,512]{2,1,0:T(2,128)S(1)} %collective-permute-done.2, f32[64,16,512]{2,1,0:T(8,128)S(1)} %copy-done.1, f32[64,16,510]{2,1,0:T(8,128)} %get-tuple-element.74, ...), kind=kOutput, calls=%fused_computation.95 | convolution fusion | flops 223346688 | bytes 27011596 | tf_op jit(solution)/shard_map/ajx,anjp->nxp/dot_general | solution.py:74
  184.6 9.1 %convolution_multiply_fusion.4 = f32[8,64,128]{2,1,0:T(8,128)S(1)} fusion(f32[8,64,2048]{2,1,0:T(8,128)} %reshape.126, f32[8,128]{1,0:T(8,128)S(1)} %copy-done.24, f32[8,2048,128]{2,1,0:T(8,128)} %gather_fusion, pred[8]{0:T(512)(128)(4,1)S(1)} %compare_and_fusion), kind=kOutput, calls=%fused_computation.152 | convolution fusion | flops 1612775424 | bytes 12849160 | tf_op jit(solution)/shard_map/anq,aqf->anf/dot_general | solution.py:71
  193.7 12.7 %fusion.151 = f32[8,64,2048]{2,1,0:T(8,128)} fusion(f32[8,64,128]{2,1,0:T(8,128)S(1)} %convolution_multiply_fusion.4, f32[8,2048,128]{2,1,0:T(8,128)} %gather_fusion, pred[8]{0:T(512)(128)(4,1)S(1)} %compare_and_fusion), kind=kOutput, calls=%fused_computation.241 | convolution fusion | flops 1612709888 | bytes 12845064 | tf_op jit(solution)/shard_map/anf,aqf->anq/dot_general | solution.py:72
  220.0 12.3 %fusion.50 = f32[64,16,512]{2,1,0:T(8,128)S(1)} fusion(f32[64,16,512]{2,1,0:T(8,128)S(1)} %copy-done.6, f32[64,2,512]{2,1,0:T(2,128)S(1)} %collective-permute-done.5, f32[64,2,512]{2,1,0:T(2,128)S(1)} %collective-permute-done.4, f32[64,16,512]{2,1,0:T(8,128)S(1)} %copy-done.10, f32[64,16,510]{2,1,0:T(8,128)} %get-tuple-element.64, ...), kind=kOutput, calls=%fused_computation.82 | convolution fusion | flops 223346688 | bytes 27011596 | tf_op jit(solution)/shard_map/ajx,anjp->nxp/dot_general | solution.py:74
  254.0 9.0 %convolution_multiply_fusion.3 = f32[8,64,128]{2,1,0:T(8,128)S(1)} fusion(f32[8,64,2048]{2,1,0:T(8,128)} %reshape.128, f32[8,128]{1,0:T(8,128)S(1)} %copy-done.24, f32[8,2048,128]{2,1,0:T(8,128)} %gather_fusion, pred[8]{0:T(512)(128)(4,1)S(1)} %compare_and_fusion), kind=kOutput, calls=%fused_computation.151 | convolution fusion | flops 1612775424 | bytes 12849160 | tf_op jit(solution)/shard_map/anq,aqf->anf/dot_general | solution.py:71
  263.0 12.7 %fusion.150 = f32[8,64,2048]{2,1,0:T(8,128)} fusion(f32[8,64,128]{2,1,0:T(8,128)S(1)} %convolution_multiply_fusion.3, f32[8,2048,128]{2,1,0:T(8,128)} %gather_fusion, pred[8]{0:T(512)(128)(4,1)S(1)} %compare_and_fusion), kind=kOutput, calls=%fused_computation.240 | convolution fusion | flops 1612709888 | bytes 12845064 | tf_op jit(solution)/shard_map/anf,aqf->anq/dot_general | solution.py:72
  289.2 13.8 %fusion.37 = f32[64,16,512]{2,1,0:T(8,128)S(1)} fusion(f32[64,16,512]{2,1,0:T(8,128)} %copy-done.2, f32[64,2,512]{2,1,0:T(2,128)S(1)} %collective-permute-done.7, f32[64,2,512]{2,1,0:T(2,128)S(1)} %collective-permute-done.6, f32[64,16,512]{2,1,0:T(8,128)S(1)} %copy-done.7, f32[64,16,510]{2,1,0:T(8,128)} %get-tuple-element.54, ...), kind=kOutput, calls=%fused_computation.69 | convolution fusion | flops 223346688 | bytes 27011596 | tf_op jit(solution)/shard_map/ajx,anjp->nxp/dot_general | solution.py:74
  324.6 9.3 %convolution_multiply_fusion.2 = f32[8,64,128]{2,1,0:T(8,128)S(1)} fusion(f32[8,64,2048]{2,1,0:T(8,128)} %reshape.130, f32[8,128]{1,0:T(8,128)S(1)} %copy-done.24, f32[8,2048,128]{2,1,0:T(8,128)} %gather_fusion, pred[8]{0:T(512)(128)(4,1)S(1)} %compare_and_fusion), kind=kOutput, calls=%fused_computation.150 | convolution fusion | flops 1612775424 | bytes 12849160 | tf_op jit(solution)/shard_map/anq,aqf->anf/dot_general | solution.py:71
  333.8 12.7 %fusion.149 = f32[8,64,2048]{2,1,0:T(8,128)} fusion(f32[8,64,128]{2,1,0:T(8,128)S(1)} %convolution_multiply_fusion.2, f32[8,2048,128]{2,1,0:T(8,128)} %gather_fusion, pred[8]{0:T(512)(128)(4,1)S(1)} %compare_and_fusion), kind=kOutput, calls=%fused_computation.239 | convolution fusion | flops 1612709888 | bytes 12845064 | tf_op jit(solution)/shard_map/anf,aqf->anq/dot_general | solution.py:72
  359.9 12.0 %fusion.24 = f32[64,16,512]{2,1,0:T(8,128)S(1)} fusion(f32[64,16,512]{2,1,0:T(8,128)S(1)} %fusion.37, f32[64,2,512]{2,1,0:T(2,128)S(1)} %collective-permute-done.9, f32[64,2,512]{2,1,0:T(2,128)S(1)} %collective-permute-done.8, f32[64,16,512]{2,1,0:T(8,128)S(1)} %copy-done.3, f32[64,16,510]{2,1,0:T(8,128)} %get-tuple-element.44, ...), kind=kOutput, calls=%fused_computation.56 | convolution fusion | flops 223346688 | bytes 27011596 | tf_op jit(solution)/shard_map/ajx,anjp->nxp/dot_general | solution.py:74
  393.5 9.1 %convolution_multiply_fusion.1 = f32[8,64,128]{2,1,0:T(8,128)S(1)} fusion(f32[8,64,2048]{2,1,0:T(8,128)} %reshape.132, f32[8,128]{1,0:T(8,128)S(1)} %copy-done.24, f32[8,2048,128]{2,1,0:T(8,128)} %gather_fusion, pred[8]{0:T(512)(128)(4,1)S(1)} %compare_and_fusion), kind=kOutput, calls=%fused_computation.149 | convolution fusion | flops 1612775424 | bytes 12849160 | tf_op jit(solution)/shard_map/anq,aqf->anf/dot_general | solution.py:71
  402.6 12.8 %fusion.148 = f32[8,64,2048]{2,1,0:T(8,128)} fusion(f32[8,64,128]{2,1,0:T(8,128)S(1)} %convolution_multiply_fusion.1, f32[8,2048,128]{2,1,0:T(8,128)} %gather_fusion, pred[8]{0:T(512)(128)(4,1)S(1)} %compare_and_fusion), kind=kOutput, calls=%fused_computation.238 | convolution fusion | flops 1612709888 | bytes 12845064 | tf_op jit(solution)/shard_map/anf,aqf->anq/dot_general | solution.py:72
  428.6 12.9 %fusion.11 = f32[64,16,512]{2,1,0:T(8,128)} fusion(f32[64,16,512]{2,1,0:T(8,128)S(1)} %copy-done.12, f32[64,2,512]{2,1,0:T(2,128)S(1)} %collective-permute-done.11, f32[64,2,512]{2,1,0:T(2,128)S(1)} %collective-permute-done.10, f32[64,16,512]{2,1,0:T(8,128)S(1)} %fusion.37, f32[64,16,510]{2,1,0:T(8,128)} %get-tuple-element.34, ...), kind=kOutput, calls=%fused_computation.43 | convolution fusion | flops 223346688 | bytes 27011596 | tf_op jit(solution)/shard_map/ajx,anjp->nxp/dot_general | solution.py:74
  444.7 55.2 %all_to_all.19 = f32[64,8,1024]{2,0,1:T(8,128)S(1)} all-to-all(f32[64,8,1024]{2,0,1:T(8,128)S(1)} %copy.29), channel_id=1, replica_groups=mesh['band'=8,'slab'=4] {'band'}, dimensions={1} | all-to-all | bytes 4194304 | tf_op jit(solution)/shard_map/all_to_all | solution.py:94
  504.6 34.8 %all-reduce.52.cloned.1.call-done = f32[512,512]{0,1:T(8,128)} async-done(((f32[512,512]{0,1:T(8,128)}), f32[512,512]{0,1:T(8,128)}) %all-reduce.52.cloned.1.call-update) | async-done | bytes 1048592 | tf_op jit(solution)/shard_map/psum | solution.py:97
  540.8 80.9 %all-reduce.54.cloned.1.call-done = f32[512,512]{0,1:T(8,128)} async-done(((f32[512,512]{0,1:T(8,128)}), f32[512,512]{0,1:T(8,128)}) %all-reduce.54.cloned.1.call-update) | async-done | bytes 1048592 | tf_op jit(solution)/shard_map/psum | solution.py:97
  623.6 11.7 %cholesky.104 = f32[128,128]{1,0:T(8,128)S(1)} custom-call(f32[128,128]{1,0:T(8,128)S(1)} %cholesky.266), custom_call_target="Cholesky" | custom-call | tf_op jit(solution)/shard_map/jit(cholesky)/cholesky | solution.py:98
  635.5 9.8 %custom-call.31 = f32[1,128,128]{1,2,0:T(8,128)S(1)} custom-call(f32[1,128,128]{2,1,0:T(8,128)S(1)} %get-tuple-element.96), custom_call_target="InvertDiagBlocksLowerTriangular" | custom-call | tf_op jit(solution)/shard_map/jit(cholesky)/cholesky | solution.py:98
  646.0 11.7 %cholesky.217 = f32[128,128]{1,0:T(8,128)S(1)} custom-call(f32[128,128]{1,0:T(8,128)S(1)} %cholesky.270), custom_call_target="Cholesky" | custom-call | tf_op jit(solution)/shard_map/jit(cholesky)/cholesky | solution.py:98
  659.1 10.0 %custom-call.32 = f32[1,128,128]{1,2,0:T(8,128)S(1)} custom-call(f32[1,128,128]{2,1,0:T(8,128)S(1)} %get-tuple-element.93), custom_call_target="InvertDiagBlocksLowerTriangular" | custom-call | tf_op jit(solution)/shard_map/jit(cholesky)/cholesky | solution.py:98
  669.7 11.7 %cholesky.238 = f32[128,128]{1,0:T(8,128)S(1)} custom-call(f32[128,128]{1,0:T(8,128)S(1)} %cholesky.275), custom_call_target="Cholesky" | custom-call | tf_op jit(solution)/shard_map/jit(cholesky)/cholesky | solution.py:98
  682.2 9.8 %custom-call.33 = f32[1,128,128]{1,2,0:T(8,128)S(1)} custom-call(f32[1,128,128]{2,1,0:T(8,128)S(1)} %get-tuple-element.90), custom_call_target="InvertDiagBlocksLowerTriangular" | custom-call | tf_op jit(solution)/shard_map/jit(cholesky)/cholesky | solution.py:98
  692.6 11.9 %cholesky.255 = f32[128,128]{1,0:T(8,128)S(1)} custom-call(f32[128,128]{1,0:T(8,128)S(1)} %convolution_subtract_fusion.4), custom_call_target="Cholesky" | custom-call | tf_op jit(solution)/shard_map/jit(cholesky)/cholesky | solution.py:98
  708.0 8.2 %while.1 = (s32[]{:T(128)}, f32[512,512]{1,0:T(8,128)S(1)}, s32[4,2]{0,1:T(2,128)S(1)}, f32[4,128,128]{2,1,0:T(8,128)S(1)}, s32[]{:T(128)}) while((s32[]{:T(128)}, f32[512,512]{1,0:T(8,128)S(1)}, s32[4,2]{0,1:T(2,128)S(1)}, f32[4,128,128]{2,1,0:T(8,128)S(1)}, s32[]{:T(128)}) %tuple.61), condition=%wide.while_cond, body=%wide.while_body.sunk | while | flops 2 | bytes 131181 | solution.py:99
  716.2 39.3 %custom-call.34 = f32[4,128,128]{1,2,0:T(8,128)S(1)} custom-call(f32[4,128,128]{2,1,0:T(8,128)S(1)} %get-tuple-element.12), custom_call_target="InvertDiagBlocksLowerTriangular" | custom-call | tf_op jit(solution)/shard_map/jit(_solve_triangular)/triangular_solve | solution.py:99
  (191 shorter events, 245.8 us)
Async XLA Ops:
  6.5 532.9 %all-reduce.52.cloned.1.call-start = ((), (), s32[]{:S(2)}) async-start(), calls=%async_computation.1 | async-start | bytes 2097152 | tf_op jit(solution)/shard_map/psum | solution.py:97
  8.3 70.2 %collective-permute-start.1 = (f32[64,2,512]{2,1,0:T(2,128)S(1)}, f32[64,2,512]{2,1,0:T(2,128)S(1)}, u32[]{:S(2)}, u32[]{:S(2)}) collective-permute-start(f32[64,2,512]{2,1,0:T(2,128)S(1)} %get-tuple-element.85), channel_id=1, source_target_pairs={{1,0},{2,1},{3,2},{0,3},{5,4},{6,5},{7,6},{4,7},{9,8},{10,9},{11,1... | collective-permute-start | bytes 786440 | tf_op jit(solution)/shard_map/ppermute | solution.py:23
  10.8 67.9 %collective-permute-start = (f32[64,2,512]{2,1,0:T(2,128)S(1)}, f32[64,2,512]{2,1,0:T(2,128)S(1)}, u32[]{:S(2)}, u32[]{:S(2)}) collective-permute-start(f32[64,2,512]{2,1,0:T(2,128)S(1)} %get-tuple-element.86), channel_id=1, source_target_pairs={{0,1},{1,2},{2,3},{3,0},{4,5},{5,6},{6,7},{7,4},{8,9},{9,10},{10,1... | collective-permute-start | bytes 786440 | tf_op jit(solution)/shard_map/ppermute | solution.py:22
  44.4 6.6 copy-start.24
  51.0 10.4 %copy-start = (f32[8,2048,128]{2,1,0:T(8,128)S(1)}, f32[8,2048,128]{2,1,0:T(8,128)}, u32[]{:S(2)}) copy-start(f32[8,2048,128]{2,1,0:T(8,128)} %gather_fusion) | copy-start | bytes 25165828
  93.7 10.6 %copy-start.8 = (f32[64,16,512]{2,1,0:T(8,128)}, f32[64,16,512]{2,1,0:T(8,128)S(1)}, u32[]{:S(2)}) copy-start(f32[64,16,512]{2,1,0:T(8,128)S(1)} %fusion.75) | copy-start | bytes 6291460
  143.5 7.2 collective-permute-start.2
  144.2 6.5 copy-start.9
  144.2 6.5 copy-start.19
  144.3 6.5 collective-permute-start.3
  162.8 10.7 %copy-start.4 = (f32[64,16,512]{2,1,0:T(8,128)}, f32[64,16,512]{2,1,0:T(8,128)S(1)}, u32[]{:S(2)}) copy-start(f32[64,16,512]{2,1,0:T(8,128)S(1)} %fusion.63) | copy-start | bytes 6291460
  206.4 8.2 %copy-start.5 = (f32[64,16,512]{2,1,0:T(8,128)S(1)}, f32[64,16,512]{2,1,0:T(8,128)}, u32[]{:S(2)}) copy-start(f32[64,16,512]{2,1,0:T(8,128)} %copy-done.4) | copy-start | bytes 6291460
  212.6 7.4 collective-permute-start.4
  213.8 6.2 copy-start.6
  213.8 6.2 copy-start.10
  213.8 6.2 copy-start.17
  213.8 6.2 collective-permute-start.5
  232.3 51.4 %copy-start.2 = (f32[64,16,512]{2,1,0:T(8,128)}, f32[64,16,512]{2,1,0:T(8,128)S(1)}, u32[]{:S(2)}) copy-start(f32[64,16,512]{2,1,0:T(8,128)S(1)} %fusion.50) | copy-start | bytes 6291460
  281.8 7.4 collective-permute-start.6
  283.0 6.2 copy-start.7
  283.0 6.2 copy-start.16
  283.0 6.2 collective-permute-start.7
  352.6 7.3 collective-permute-start.8
  353.7 6.2 copy-start.3
  353.7 6.2 copy-start.18
  353.7 6.1 collective-permute-start.9
  371.8 10.6 %copy-start.11 = (f32[64,16,512]{2,1,0:T(8,128)}, f32[64,16,512]{2,1,0:T(8,128)S(1)}, u32[]{:S(2)}) copy-start(f32[64,16,512]{2,1,0:T(8,128)S(1)} %fusion.24) | copy-start | bytes 6291460
  421.4 7.2 collective-permute-start.10
  422.6 6.1 collective-permute-start.11
  504.4 117.3 %all-reduce.54.cloned.1.call-start = ((), (), s32[]{:S(2)}) async-start(), calls=%async_computation.2 | async-start | bytes 2097152 | tf_op jit(solution)/shard_map/psum | solution.py:97
  704.5 52.7 %copy-start.21 = (f32[2,64,1024]{2,1,0:T(8,128)S(1)}, f32[2,64,1024]{2,1,0:T(8,128)}, u32[]{:S(2)}) copy-start(f32[2,64,1024]{2,1,0:T(8,128)} %get-tuple-element.25) | copy-start | bytes 1572868
  716.2 42.3 %copy-start.20 = (f32[2,64,1024]{2,1,0:T(8,128)S(1)}, f32[2,64,1024]{2,1,0:T(8,128)}, u32[]{:S(2)}) copy-start(f32[2,64,1024]{2,1,0:T(8,128)} %get-tuple-element.24) | copy-start | bytes 1572868
  (8 other events, 29.7 us)
Sparse Core Ops, SparseCore 0:
  504.5 34.8 all-reduce.51
  542.9 78.7 all-reduce.53
